TPU v7x, 128 devices: a whole 4x4x4 slice. The times are simulated.
128 devices in a mesh: ex: 16 (over x, z), tp: 4 (over y), dp: 2 (over core).
Axes of the slice: x: 4, y: 4, z: 4, core: 2. Of those that a mesh axis runs over, the one named last changes fastest.
Arguments:
- tokens: bfloat16 [4096, 2880], P(('ex', 'dp')), may hold values from -32 to 32
- route_one: int32 [4096, 4], P(('ex', 'dp')), may hold values from 0 to 15, as said below
- route_two: int32 [4096, 4], P(('ex', 'dp')), may hold values from 0 to 15, as said below
- share_one: float32 [4096, 4], P(('ex', 'dp')), may hold values from 0.05 to 0.6
- share_two: float32 [4096, 4], P(('ex', 'dp')), may hold values from 0.05 to 0.6
- gain_one: float32 [2880], replicated, may hold values from 0.5 to 1.5
- gain_two: float32 [2880], replicated, may hold values from 0.5 to 1.5
- gate_up_one: bfloat16 [16, 2880, 2, 2880], P('ex', None, None, 'tp'), may hold values from -0.109375 to 0.109375
- down_one: bfloat16 [16, 2880, 2880], P('ex', 'tp'), may hold values from -0.109375 to 0.109375
- gate_up_two: bfloat16 [16, 2880, 2, 2880], P('ex', None, None, 'tp'), may hold values from -0.109375 to 0.109375
- down_two: bfloat16 [16, 2880, 2880], P('ex', 'tp'), may hold values from -0.109375 to 0.109375
Outputs:
- mixed: bfloat16 [4096, 2880], P(('ex', 'dp'), 'tp')
- load: int32 [2, 16], P(None, 'ex')
Inputs may be any that keep to these rules, and one draw needn't show every extreme that they name: `route_one`: each row names 4 different experts; in each aligned block of 128 rows no expert is named by more than 64 rows, and in every block some expert is named by exactly 64 rows. `route_two`: each row names 4 different experts; in each aligned block of 128 rows no expert is named by more than 64 rows, and in every block some expert is named by exactly 64 rows.
All inputs are finite; a program needn't handle non-finite values.
Results may differ from a plain program's by a relative error of at most 0.011.
Values may be sent and summed in bfloat16 or wider, within the bound.
A program may use at most 128 MiB of HBM per device.

v0:
```python
import jax
import jax.numpy as jnp
from jax import lax
from jax.sharding import PartitionSpec as P

norm_eps = 1e-05
glu_alpha = 1.702


def cut_along(value, dim, length):
    before, after = (value.shape[:dim], value.shape[dim + 1 :])
    return jnp.moveaxis(value.reshape(*before, length, -1, *after), dim, 0)


def sent_and_summed(value, axis, dim):
    length = lax.axis_size(axis)
    pieces = lax.all_to_all(cut_along(value, dim, length), axis, 0, 0, tiled=True)
    return jnp.sum(pieces.astype(jnp.float32), axis=0)


def normalize(stream, gains):
    values = stream.astype(jnp.float32)
    inverse = lax.rsqrt(jnp.mean(values * values, axis=1, keepdims=True) + norm_eps)
    return (values * inverse * gains[None, :]).astype(jnp.bfloat16)


def placement(routes, experts, capacity):
    tokens_here = routes.shape[0]
    top_count = routes.shape[1]
    flattened = routes.reshape(tokens_here * top_count)
    matches = (flattened[:, None] == jnp.arange(experts, dtype=jnp.int32)[None, :]).astype(
        jnp.int32
    )
    slot_rank = jnp.cumsum(matches, axis=0) - 1
    slot_index = jnp.sum(slot_rank * matches, axis=1)
    target = (flattened * capacity + slot_index).reshape(tokens_here, top_count)
    return (target, jnp.sum(matches, axis=0))


def pack_rows(target, normed, total_slots):
    wanted = jnp.arange(total_slots, dtype=jnp.int32)[:, None, None] == target[None, :, :]
    chooser = jnp.any(wanted, axis=2).astype(jnp.bfloat16)
    return jnp.dot(chooser, normed, preferred_element_type=jnp.float32).astype(jnp.bfloat16)


def activate(hidden, share_width):
    gate_part = hidden[..., :share_width]
    up_part = hidden[..., share_width:]
    return (gate_part * jax.nn.sigmoid(glu_alpha * gate_part) * (up_part + 1.0)).astype(
        jnp.bfloat16
    )


def expert_layer(stream, routes, shares, gains, gate_up, down_proj):
    ex_count = lax.axis_size("ex")
    tp_count = lax.axis_size("tp")
    tp_place = lax.axis_index("tp")
    local_count = gate_up.shape[0]
    model_width = gate_up.shape[1]
    share_width = gate_up.shape[3]
    experts = local_count * ex_count
    tokens_here = routes.shape[0]
    top_count = routes.shape[1]
    capacity = 2 * tokens_here * top_count // experts
    col_share = model_width // tp_count
    normed = normalize(stream, gains)
    target, counted = placement(routes, experts, capacity)
    gate_up_flat = gate_up.reshape(local_count, model_width, 2 * share_width)
    counts_out = counted.reshape(ex_count, local_count)
    packed = pack_rows(target, normed, experts * capacity).reshape(
        ex_count, local_count, capacity, model_width
    )
    arrived, arrived_counts = (
        lax.all_to_all(packed, "ex", split_axis=0, concat_axis=0, tiled=True),
        lax.all_to_all(counts_out, "ex", split_axis=0, concat_axis=0, tiled=True),
    )
    hidden = jnp.einsum("secd,edf->secf", arrived, gate_up_flat, preferred_element_type=jnp.float32)
    activated = activate(hidden, share_width)
    partial_value = jnp.einsum(
        "secf,efd->secd", activated, down_proj, preferred_element_type=jnp.float32
    )
    partial_value = lax.optimization_barrier(partial_value.astype(jnp.bfloat16)).astype(jnp.float32)
    resident = stream.astype(jnp.float32)
    expert_rows = sent_and_summed(partial_value.astype(jnp.bfloat16), "tp", 3).astype(jnp.bfloat16)
    returned = lax.all_to_all(expert_rows, "ex", split_axis=0, concat_axis=0, tiled=True)
    residual = lax.dynamic_slice_in_dim(resident, tp_place * col_share, col_share, 1)
    out_width = returned.shape[3]
    flat_returned = returned.reshape(experts * capacity, out_width)
    picked = jnp.take(flat_returned, target.reshape(tokens_here * top_count), axis=0)
    picked = picked.reshape(tokens_here, top_count, out_width).astype(jnp.float32)
    mixed = residual + jnp.sum(shares[:, :, None] * picked, axis=1)
    return (mixed.astype(jnp.bfloat16), jnp.sum(arrived_counts, axis=0))


def body(
    tokens,
    route_one,
    route_two,
    share_one,
    share_two,
    gain_one,
    gain_two,
    gate_up_one,
    down_one,
    gate_up_two,
    down_two,
):
    first_out, load_first = expert_layer(
        tokens, route_one, share_one, gain_one, gate_up_one, down_one
    )
    stream = lax.all_gather(first_out, "tp", axis=1, tiled=True)
    second, load_second = expert_layer(
        stream, route_two, share_two, gain_two, gate_up_two, down_two
    )
    load_pair = lax.psum(jnp.stack([load_first, load_second]), "dp").astype(jnp.int32)
    return (second, load_pair)


def solution(mesh):
    in_specs = (
        P(("ex", "dp"), None),
        P(("ex", "dp"), None),
        P(("ex", "dp"), None),
        P(("ex", "dp"), None),
        P(("ex", "dp"), None),
        P(),
        P(),
        P("ex", None, None, "tp"),
        P("ex", "tp", None),
        P("ex", None, None, "tp"),
        P("ex", "tp", None),
    )
    out_specs = (P(("ex", "dp"), "tp"), P(None, "ex"))
    return jax.shard_map(body, mesh=mesh, in_specs=in_specs, out_specs=out_specs, check_vma=False)
```

profile of v0, /device:TPU:0, one launch (start us, length us, event | category | flops | bytes accessed | tf_op | source)
XLA Modules:
  0.0 517.0 jit_solution(11135436432430650114)
XLA Ops:
  0.6 0.8 copy.107
  1.6 1.2 reduce-window.14
  2.8 0.2 slice_reduce_fusion.1
  3.1 0.2 convert_reduce_fusion.1
  3.4 0.7 multiply_add_fusion.1
  4.1 0.4 fusion.16
  4.5 1.5 copy.105
  5.9 0.2 multiply_reduce_fusion.3
  6.2 5.1 convolution_convert_fusion.1
  11.2 8.5 %copy.111 = bf16[1024,2880]{1,0:T(8,128)(2,1)} copy(bf16[1024,2880]{0,1:T(8,128)(2,1)} %convolution_convert_fusion.1) | data formatting | bytes 11796480 | tf_op jit(solution)/shard_map/convert_element_type | solution.py:43
  19.8 79.3 %all_to_all.48 = bf16[16,1,64,2880]{3,2,1,0:T(8,128)(2,1)S(1)} all-to-all(bf16[16,1,64,2880]{3,2,1,0:T(8,128)(2,1)} %bitcast.121), channel_id=1, replica_groups=mesh['ex'=16,'tp'=4,'dp'=2] {'ex'}, dimensions={0} | all-to-all | bytes 11796480 | tf_op jit(solution)/shard_map/all_to_all | solution.py:74
  99.0 12.5 %fusion.4 = f32[16,1,64,1440]{3,2,0,1:T(8,128)S(1)} fusion(bf16[2880,1440,1]{0,1,2:T(8,128)(2,1)} %bitcast.126, bf16[16,1,64,2880]{3,2,1,0:T(8,128)(2,1)S(1)} %all_to_all.48), kind=kOutput, calls=%fused_computation.12 | convolution fusion | flops 8493465600 | bytes 20090880 | tf_op jit(solution)/shard_map/secd,edf->secf/dot_general | solution.py:77
  111.5 7.4 %convert_bitcast_fusion.1 = bf16[16,1,64,2880]{3,2,0,1:T(8,128)(2,1)} fusion(bf16[1,720,2880]{2,1,0:T(8,128)(2,1)S(1)} %bitcast.129, f32[16,1,64,1440]{3,2,0,1:T(8,128)S(1)} %fusion.4), kind=kOutput, calls=%fused_computation.9 | convolution fusion | flops 4255580160 | bytes 15943680 | tf_op jit(solution)/shard_map/secf,efd->secd/dot_general | solution.py:79
  118.9 15.2 %reshape.159 = bf16[16,1,64,4,720]{4,3,2,0,1:T(4,128)(2,1)} reshape(bf16[16,1,64,2880]{3,2,0,1:T(8,128)(2,1)} %convert_bitcast_fusion.1) | data formatting | bytes 11796480 | tf_op jit(solution)/shard_map/reshape | solution.py:12
  134.1 3.9 copy.134
  138.0 74.2 %all_to_all.49 = bf16[4,16,1,64,720]{4,3,1,2,0:T(8,128)(2,1)} all-to-all(bf16[4,16,1,64,720]{4,3,1,2,0:T(8,128)(2,1)S(1)} %bitcast.119), channel_id=1, replica_groups=mesh['ex'=16,'tp'=4,'dp'=2] {'tp'}, dimensions={0} | all-to-all | bytes 11796480 | tf_op jit(solution)/shard_map/all_to_all | solution.py:17
  212.2 5.6 %reduce_sum.125 = bf16[16,64,720]{2,1,0:T(8,128)(2,1)} reduce(bf16[4,16,1,64,720]{4,3,1,2,0:T(8,128)(2,1)} %all_to_all.49, bf16[]{:T(256)} %constant.50.clone.1), dimensions={0,2}, to_apply=%region_5.6 | reduce | flops 2211840 | bytes 7372802 | tf_op jit(solution)/shard_map/reduce_sum | solution.py:18
  217.8 4.3 all-to-all-start.2
  222.1 1.3 convert_element_type.92
  223.7 0.1 copy.106
  223.8 1.2 reduce-window.16
  225.0 0.2 slice_reduce_fusion
  225.2 0.2 convert_reduce_fusion
  225.6 0.4 fusion.17
  226.0 16.8 %all-to-all-done.2 = bf16[16,1,64,720]{3,2,1,0:T(8,128)(2,1)S(1)} async-done(((bf16[16,1,64,720]{3,2,1,0:T(8,128)(2,1)}), bf16[16,1,64,720]{3,2,1,0:T(8,128)(2,1)S(1)}, u32[]{:S(2)}, u32[]{:S(2)}) %all-to-all-start.2) | async-done | bytes 1474592 | tf_op jit(solution)/shard_map/all_to_all | solution.py:85
  242.8 2.0 gather_fusion
  244.8 0.2 select_convert_fusion.1
  245.0 0.5 reshape.169
  245.5 1.0 multiply_reduce_fusion.1
  246.5 1.2 add_convert_fusion.1
  247.7 0.2 copy.114
  247.9 13.6 %all_gather.3 = bf16[128,2880]{0,1:T(8,128)(2,1)S(1)} all-gather(bf16[128,720]{0,1:T(8,128)(2,1)S(1)} %copy.114), channel_id=1, replica_groups=mesh['ex'=16,'tp'=4,'dp'=2] {'tp'}, dimensions={1}, use_global_device_ids=true | all-gather | bytes 921600 | tf_op jit(solution)/shard_map/all_gather | solution.py:111
  261.5 0.3 copy.115
  261.8 0.2 multiply_reduce_fusion.2
  262.1 4.4 convolution_convert_fusion
  266.4 8.5 %copy.121 = bf16[1024,2880]{1,0:T(8,128)(2,1)} copy(bf16[1024,2880]{0,1:T(8,128)(2,1)} %convolution_convert_fusion) | data formatting | bytes 11796480 | tf_op jit(solution)/shard_map/convert_element_type | solution.py:43
  275.0 4.8 all-to-all-start.3
  279.7 0.7 copy.124
  280.4 71.2 %all-to-all-done.3 = bf16[16,1,64,2880]{3,2,1,0:T(8,128)(2,1)} async-done(((bf16[16,1,64,2880]{3,2,1,0:T(8,128)(2,1)}), bf16[16,1,64,2880]{3,2,1,0:T(8,128)(2,1)}, u32[]{:S(2)}, u32[]{:S(2)}) %all-to-all-start.3) | async-done | bytes 5898272 | tf_op jit(solution)/shard_map/all_to_all | solution.py:74
  351.6 5.7 %all-to-all-start.6 = ((s32[16,1,1]{2,1,0:T(1,128)}), s32[16,1,1]{2,1,0:T(1,128)S(1)}, u32[]{:S(2)}, u32[]{:S(2)}) async-start(s32[16,1,1]{2,1,0:T(1,128)} %copy.124), calls=%async_computation.6 | async-start | bytes 16384 | tf_op jit(solution)/shard_map/all_to_all | solution.py:75
  357.4 14.4 %fusion.7 = f32[16,1,64,1440]{3,2,0,1:T(8,128)S(1)} fusion(bf16[2880,1440,1]{0,1,2:T(8,128)(2,1)} %bitcast.127, bf16[16,1,64,2880]{3,2,1,0:T(8,128)(2,1)} %all-to-all-done.3), kind=kOutput, calls=%fused_computation.13 | convolution fusion | flops 8493465600 | bytes 20090880 | tf_op jit(solution)/shard_map/secd,edf->secf/dot_general | solution.py:77
  371.8 7.3 %convert_bitcast_fusion = bf16[16,1,64,2880]{3,2,0,1:T(8,128)(2,1)} fusion(bf16[1,720,2880]{2,1,0:T(8,128)(2,1)S(1)} %bitcast.131, f32[16,1,64,1440]{3,2,0,1:T(8,128)S(1)} %fusion.7), kind=kOutput, calls=%fused_computation.8 | convolution fusion | flops 4255580160 | bytes 15943680 | tf_op jit(solution)/shard_map/secf,efd->secd/dot_general | solution.py:79
  379.1 15.2 %reshape.167 = bf16[16,1,64,4,720]{4,3,2,0,1:T(4,128)(2,1)} reshape(bf16[16,1,64,2880]{3,2,0,1:T(8,128)(2,1)} %convert_bitcast_fusion) | data formatting | bytes 11796480 | tf_op jit(solution)/shard_map/reshape | solution.py:12
  394.3 6.6 %copy.133 = bf16[16,1,64,4,720]{4,2,0,1,3:T(8,128)(2,1)} copy(bf16[16,1,64,4,720]{4,3,2,0,1:T(4,128)(2,1)} %reshape.167) | data formatting | bytes 11796480 | tf_op jit(solution)/shard_map/reshape | solution.py:12
  400.9 5.2 %all-to-all-start.4 = ((bf16[4,16,1,64,720]{4,3,1,2,0:T(8,128)(2,1)}), bf16[4,16,1,64,720]{4,3,1,2,0:T(8,128)(2,1)}, u32[]{:S(2)}, u32[]{:S(2)}) async-start(bf16[4,16,1,64,720]{4,3,1,2,0:T(8,128)(2,1)} %bitcast.118), calls=%async_computation.4 | async-start | bytes 12582912 | tf_op jit(solution)/shard_map/all_to_all | solution.py:17
  406.2 0.7 copy.125
  406.9 67.0 %all-to-all-done.4 = bf16[4,16,1,64,720]{4,3,1,2,0:T(8,128)(2,1)} async-done(((bf16[4,16,1,64,720]{4,3,1,2,0:T(8,128)(2,1)}), bf16[4,16,1,64,720]{4,3,1,2,0:T(8,128)(2,1)}, u32[]{:S(2)}, u32[]{:S(2)}) %all-to-all-start.4) | async-done | bytes 5898272 | tf_op jit(solution)/shard_map/all_to_all | solution.py:17
  473.9 7.0 %all-to-all-start.7 = ((s32[16,1,1]{2,1,0:T(1,128)}), s32[16,1,1]{2,1,0:T(1,128)S(1)}, u32[]{:S(2)}, u32[]{:S(2)}) async-start(s32[16,1,1]{2,1,0:T(1,128)} %copy.125), calls=%async_computation.7 | async-start | bytes 16384 | tf_op jit(solution)/shard_map/all_to_all | solution.py:75
  480.8 5.6 %reduce_sum.131 = bf16[16,64,720]{2,1,0:T(8,128)(2,1)} reduce(bf16[4,16,1,64,720]{4,3,1,2,0:T(8,128)(2,1)} %all-to-all-done.4, bf16[]{:T(256)} %constant.50.clone.1), dimensions={0,2}, to_apply=%region_12.14 | reduce | flops 2211840 | bytes 7372802 | tf_op jit(solution)/shard_map/reduce_sum | solution.py:18
  486.4 1.9 all-to-all-done.7
  488.3 5.4 %all-to-all-start.5 = ((bf16[16,1,64,720]{3,2,1,0:T(8,128)(2,1)}), bf16[16,1,64,720]{3,2,1,0:T(8,128)(2,1)S(1)}, u32[]{:S(2)}, u32[]{:S(2)}) async-start(bf16[16,1,64,720]{3,2,1,0:T(8,128)(2,1)} %bitcast.123), calls=%async_computation.5 | async-start | bytes 3145728 | tf_op jit(solution)/shard_map/all_to_all | solution.py:85
  493.8 0.7 reduce_sum.135
  494.5 0.6 reduce_sum.137
  495.1 1.4 pad_add_fusion
  496.5 0.1 copy.116
  496.6 2.3 psum.7
  498.9 1.3 convert_element_type.104
  500.2 11.1 %all-to-all-done.5 = bf16[16,1,64,720]{3,2,1,0:T(8,128)(2,1)S(1)} async-done(((bf16[16,1,64,720]{3,2,1,0:T(8,128)(2,1)}), bf16[16,1,64,720]{3,2,1,0:T(8,128)(2,1)S(1)}, u32[]{:S(2)}, u32[]{:S(2)}) %all-to-all-start.5) | async-done | bytes 1474592 | tf_op jit(solution)/shard_map/all_to_all | solution.py:85
  511.3 2.0 gather_fusion.1
  513.3 0.2 select_convert_fusion
  513.5 0.5 reshape.170
  514.0 1.0 multiply_reduce_fusion
  515.0 1.2 add_convert_fusion
  516.2 0.8 copy.126
  (41 shorter events, 1.1 us)
Async XLA Ops:
  19.8 91.8 %slice-start = ((s8[4239360]{0:T(1024)(128)(4,1)}), s8[4194304]{0:T(1024)(128)(4,1)S(1)}, s32[]{:S(2)}) async-start(s8[4239360]{0:T(1024)(128)(4,1)} %bitcast.128), calls=%async_computation.8 | async-start | bytes 8388608
  99.0 12.5 %slice-start.1 = ((s8[4239360]{0:T(1024)(128)(4,1)}), s8[45056]{0:T(1024)(128)(4,1)S(1)}, s32[]{:S(2)}) async-start(s8[4239360]{0:T(1024)(128)(4,1)} %bitcast.128), calls=%async_computation.9 | async-start | bytes 90112
  217.8 5.6 %copy-start.1 = (s32[128,4]{0,1:T(4,128)S(1)}, s32[128,4]{0,1:T(4,128)}, u32[]{:S(2)}) copy-start(s32[128,4]{0,1:T(4,128)} %param.15) | copy-start | bytes 6148
  217.8 5.9 %copy-start.2 = (f32[128,4]{0,1:T(4,128)S(1)}, f32[128,4]{0,1:T(4,128)}, u32[]{:S(2)}) copy-start(f32[128,4]{0,1:T(4,128)} %param.16) | copy-start | bytes 6148
  217.8 25.0 %all-to-all-start.2 = ((bf16[16,1,64,720]{3,2,1,0:T(8,128)(2,1)}), bf16[16,1,64,720]{3,2,1,0:T(8,128)(2,1)S(1)}, u32[]{:S(2)}, u32[]{:S(2)}) async-start(bf16[16,1,64,720]{3,2,1,0:T(8,128)(2,1)} %bitcast.122), calls=%async_computation.2 | async-start | bytes 3145728 | tf_op jit(solution)/shard_map/all_to_all | solution.py:85
  245.5 16.6 %copy-start = (f32[2880]{0:T(1024)S(1)}, f32[2880]{0:T(1024)}, u32[]{:S(2)}) copy-start(f32[2880]{0:T(1024)} %param.19) | copy-start | bytes 34564
  275.0 96.8 %slice-start.2 = ((s8[4239360]{0:T(1024)(128)(4,1)}), s8[45056]{0:T(1024)(128)(4,1)S(1)}, s32[]{:S(2)}) async-start(s8[4239360]{0:T(1024)(128)(4,1)} %bitcast.130), calls=%async_computation.10 | async-start | bytes 90112
  275.0 76.7 %all-to-all-start.3 = ((bf16[16,1,64,2880]{3,2,1,0:T(8,128)(2,1)}), bf16[16,1,64,2880]{3,2,1,0:T(8,128)(2,1)}, u32[]{:S(2)}, u32[]{:S(2)}) async-start(bf16[16,1,64,2880]{3,2,1,0:T(8,128)(2,1)} %bitcast.120), calls=%async_computation.3 | async-start | bytes 12058624 | tf_op jit(solution)/shard_map/all_to_all | solution.py:74
  351.6 49.3 %all-to-all-start.6 = ((s32[16,1,1]{2,1,0:T(1,128)}), s32[16,1,1]{2,1,0:T(1,128)S(1)}, u32[]{:S(2)}, u32[]{:S(2)}) async-start(s32[16,1,1]{2,1,0:T(1,128)} %copy.124), calls=%async_computation.6 | async-start | bytes 16384 | tf_op jit(solution)/shard_map/all_to_all | solution.py:75
  357.4 14.4 %slice-start.3 = ((s8[4239360]{0:T(1024)(128)(4,1)}), s8[4194304]{0:T(1024)(128)(4,1)S(1)}, s32[]{:S(2)}) async-start(s8[4239360]{0:T(1024)(128)(4,1)} %bitcast.130), calls=%async_computation.11 | async-start | bytes 8388608
  400.9 72.9 %all-to-all-start.4 = ((bf16[4,16,1,64,720]{4,3,1,2,0:T(8,128)(2,1)}), bf16[4,16,1,64,720]{4,3,1,2,0:T(8,128)(2,1)}, u32[]{:S(2)}, u32[]{:S(2)}) async-start(bf16[4,16,1,64,720]{4,3,1,2,0:T(8,128)(2,1)} %bitcast.118), calls=%async_computation.4 | async-start | bytes 12582912 | tf_op jit(solution)/shard_map/all_to_all | solution.py:17
  473.9 14.5 %all-to-all-start.7 = ((s32[16,1,1]{2,1,0:T(1,128)}), s32[16,1,1]{2,1,0:T(1,128)S(1)}, u32[]{:S(2)}, u32[]{:S(2)}) async-start(s32[16,1,1]{2,1,0:T(1,128)} %copy.125), calls=%async_computation.7 | async-start | bytes 16384 | tf_op jit(solution)/shard_map/all_to_all | solution.py:75
  486.4 10.1 %copy-start.3 = (f32[128,4]{0,1:T(4,128)S(1)}, f32[128,4]{0,1:T(4,128)}, u32[]{:S(2)}) copy-start(f32[128,4]{0,1:T(4,128)} %param.17) | copy-start | bytes 6148
  488.3 23.0 %all-to-all-start.5 = ((bf16[16,1,64,720]{3,2,1,0:T(8,128)(2,1)}), bf16[16,1,64,720]{3,2,1,0:T(8,128)(2,1)S(1)}, u32[]{:S(2)}, u32[]{:S(2)}) async-start(bf16[16,1,64,720]{3,2,1,0:T(8,128)(2,1)} %bitcast.123), calls=%async_computation.5 | async-start | bytes 3145728 | tf_op jit(solution)/shard_map/all_to_all | solution.py:85
where the time goes:
time: 519 us; the launch traced here: 517 us
  blocking collectives  169 us (33%)
  waiting for transfers between devices  168 us (32%)
  local copies, waits for them, and re-layouts  69.4 us (13%)
  matrix products  51 us (10%)
  starting transfers between devices  32.4 us (6%)
  other arithmetic  25.7 us (5%)
    all_to_all x1, blocking collectives, expert_layer(): lax.all_to_all(packed, 'ex', split_axis=0, concat_axis=0, tiled=True)  79.3 us
    all_to_all x1, blocking collectives, sent_and_summed(): lax.all_to_all(cut_along(value, dim, length), axis, 0, 0, tiled=True)  74.2 us
    all_to_all x1, waiting for transfers between devices, expert_layer(): lax.all_to_all(packed, 'ex', split_axis=0, concat_axis=0, tiled=True)  71.2 us
    all_to_all x1, waiting for transfers between devices, sent_and_summed(): lax.all_to_all(cut_along(value, dim, length), axis, 0, 0, tiled=True)  67 us
    reshape x4, local copies, waits for them, and re-layouts, cut_along(): return jnp.moveaxis(value.reshape(*before, length, -1, *after), dim, 0)  40.9 us
    all_to_all x2, waiting for transfers between devices, expert_layer(): lax.all_to_all(expert_rows, 'ex', split_axis=0, concat_axis=0, tiled=True)  28 us
    dot_general x2, matrix products, expert_layer(): jnp.einsum('secd,edf->secf', arrived, gate_up_flat, preferred_element_typ...  26.9 us
    convert_element_type x2, local copies, waits for them, and re-layouts, pack_rows(): jnp.dot(chooser, normed, preferred_element_type=jnp.float32)  17 us
  transfers between devices with their start and end apart: 6, of which 5 were waited for; matrix products, arithmetic and copies ran while one was open for 11% of the time, Pallas kernels for 0%

commit v1 on v0

v1 whole, which is shorter than its diff:
```python
import functools

import jax
import jax.numpy as jnp
from jax import lax
from jax.experimental import pallas as pl
from jax.experimental.pallas import tpu as pltpu
from jax.sharding import PartitionSpec as P

MESH = pl.DeviceIdType.MESH
norm_eps = 1e-05
glu_alpha = 1.702
SIDE = 4
GROUPS = 4
NT = (((1,), (1,)), ((), ()))
TN = (((0,), (0,)), ((), ()))


def layer_kernel(last, cap, *refs):
    if last:
        (x_ref, rt_ref, st_ref, gain_ref, wgu_hbm, wd_hbm, out_ref, *scratch) = refs
    else:
        (x_ref, rt_ref, rt2_ref, st_ref, gain_ref, wgu_hbm, wd_hbm, out_ref, load_ref, *scratch) = refs
    (
        wgu, wd, normed, slots, shares, pk, arr, part, yr, half_buf, ret, acc, rs_send, rs_recv, w_sem,
        in_s, in_r, fw_s, fw_r, ex_s, ex_r, rt_s, rt_r, rs_s, rs_r, *more,
    ) = scratch
    tokens, width = x_ref.shape
    share_width = wd.shape[0]
    half_cap = cap // 2
    quarter = cap // 4
    rows = GROUPS * cap
    half_rows = GROUPS * half_cap

    me = lax.axis_index("ex")
    y = lax.axis_index("tp")
    c = lax.axis_index("dp")
    my_x, my_z = me // SIDE, me % SIDE
    odd = y % 2
    near = (y + 1 - 2 * odd + SIDE) % SIDE
    far = (y - 1 + 2 * odd + SIDE) % SIDE

    def expert_at(g, j):
        return ((my_x + j) % SIDE) * SIDE + (my_z + j + g) % SIDE

    def source_at(g, j):
        return ((my_x - j + SIDE) % SIDE) * SIDE + (my_z - j - g + 2 * SIDE) % SIDE

    def send(src, dst, s_sem, r_sem, device):
        return pltpu.make_async_remote_copy(
            src_ref=src, dst_ref=dst, send_sem=s_sem, recv_sem=r_sem, device_id=device, device_id_type=MESH
        )

    def al(v, m):
        return pl.multiple_of(v, m)

    barrier = pltpu.get_barrier_semaphore()
    for o in range(1, SIDE * GROUPS):
        pl.semaphore_signal(barrier, inc=1, device_id=(expert_at(o // 4, o % 4), y, c), device_id_type=MESH)
    for k in range(1, SIDE):
        pl.semaphore_signal(barrier, inc=1, device_id=(me, (y + k) % SIDE, c), device_id_type=MESH)
    if not last:
        pl.semaphore_signal(barrier, inc=1, device_id=(me, y, 1 - c), device_id_type=MESH)

    load_wgu = pltpu.make_async_copy(wgu_hbm, wgu, w_sem.at[0])
    load_wd = pltpu.make_async_copy(wd_hbm, wd, w_sem.at[1])
    load_wgu.start()
    load_wd.start()

    experts = slots.shape[0]
    expert_id = lax.broadcasted_iota(jnp.int32, (experts, tokens), 0)

    def chosen(table):
        hit = jnp.zeros((experts, tokens), jnp.float32)
        for k in range(table.shape[0]):
            hit = hit + jnp.where(table[k : k + 1, :] == expert_id, 1.0, 0.0)
        return hit

    table = rt_ref[...]
    hit = chosen(table)
    before = (
        lax.broadcasted_iota(jnp.int32, (tokens, tokens), 0) < lax.broadcasted_iota(jnp.int32, (tokens, tokens), 1)
    )
    rank = jnp.dot(
        hit.astype(jnp.bfloat16), jnp.where(before, 1.0, 0.0).astype(jnp.bfloat16), preferred_element_type=jnp.float32
    )
    slots[...] = jnp.where(hit > 0.5, rank, -1.0)
    weight = jnp.zeros((experts, tokens), jnp.float32)
    for k in range(table.shape[0]):
        weight = weight + jnp.where(table[k : k + 1, :] == expert_id, st_ref[k : k + 1, :], 0.0)
    shares[...] = weight

    gains = gain_ref[...]
    for r in range(0, tokens, 16):
        v = x_ref[r : r + 16, :].astype(jnp.float32)
        inverse = lax.rsqrt(jnp.mean(v * v, axis=1, keepdims=True) + norm_eps)
        normed[r : r + 16, :] = (v * inverse * gains).astype(jnp.bfloat16)

    if not last:
        hits, cnt_s_buf, cnt_r_buf, pair_s_buf, pair_r_buf, gathered, cs, cr, ag_s, ag_r = more
        hits[0] = hit
        hits[1] = chosen(rt2_ref[...])

    pl.semaphore_wait(barrier, (SIDE * GROUPS - 1) + (SIDE - 1) + (0 if last else 1))

    def in_copy(g, j, device):
        o = g * 4 + j
        at = pl.ds(al(o * cap + odd * half_cap, half_cap), half_cap)
        return send(pk.at[at], arr.at[at], in_s.at[o], in_r.at[o], device)

    slot_id = lax.broadcasted_iota(jnp.int32, (cap, tokens), 0).astype(jnp.float32)

    def pack(g, _):
        chooser = jnp.concatenate(
            [jnp.where(slots[pl.ds(expert_at(g, j), 1), :] == slot_id, 1.0, 0.0) for j in range(4)], axis=0
        ).astype(jnp.bfloat16)
        packed = jnp.dot(chooser, normed[...], preferred_element_type=jnp.float32).astype(jnp.bfloat16)
        pk[pl.ds(al(g * rows, rows), rows), :] = packed

        @pl.when(g == 0)
        def _():
            arr[0:cap, :] = packed[0:cap]

        for j in range(4):

            @pl.when(g * 4 + j > 0)
            def _():
                in_copy(g, j, (expert_at(g, j), y, c)).start()

        return 0

    lax.fori_loop(0, GROUPS, pack, 0)

    if not last:

        def count_copy(o, device):
            return send(cnt_s_buf.at[o], cnt_r_buf.at[o], cs.at[o], cr.at[o], device)

        row_id = lax.broadcasted_iota(jnp.int32, (8, 128), 0)

        def count_tile(e):
            one = jnp.sum(hits[0, pl.ds(e, 1), :], axis=1, keepdims=True)
            two = jnp.sum(hits[1, pl.ds(e, 1), :], axis=1, keepdims=True)
            return jnp.where(row_id == 0, one, jnp.where(row_id == 1, two, 0.0)).astype(jnp.int32)

        cnt_r_buf[0] = count_tile(me)
        for o in range(1, 16):
            cnt_s_buf[o] = count_tile(expert_at(o // 4, o % 4))
            count_copy(o, (expert_at(o // 4, o % 4), y, c)).start()

    def fw_copy(o, j, side):
        at = pl.ds(al(o * cap + side * half_cap + j * quarter, quarter), quarter)
        return send(arr.at[at], arr.at[at], fw_s.at[o, j], fw_r.at[o, j], (me, (near, far)[j], c))

    def forward(g):
        for j in range(4):
            o = g * 4 + j

            @pl.when(o > 0)
            def _():
                in_copy(g, j, (me, y, c)).wait_recv()
                fw_copy(o, 0, odd).start()
                fw_copy(o, 1, odd).start()

    def ex_copy(o, j, side):
        src = pl.ds(al(o * cap + side * half_cap + j * quarter, quarter), quarter)
        dst = pl.ds(al(o * half_cap + j * quarter, quarter), quarter)
        return send(part.at[src], yr.at[dst], ex_s.at[o, j], ex_r.at[o, j], (me, (near, far)[j], c))

    def experts_of(g):
        for j in range(4):
            o = g * 4 + j

            @pl.when(o > 0)
            def _():
                fw_copy(o, 0, 1 - odd).wait_recv()
                fw_copy(o, 1, 1 - odd).wait_recv()

        at = pl.ds(al(g * rows, rows), rows)
        inputs = arr[at, :]
        gate = lax.dot_general(inputs, wgu[0:share_width, :], NT, preferred_element_type=jnp.float32)
        up = lax.dot_general(inputs, wgu[share_width:, :], NT, preferred_element_type=jnp.float32)
        act = (gate * jax.nn.sigmoid(glu_alpha * gate) * (up + 1.0)).astype(jnp.bfloat16)
        part[at, :] = jnp.dot(act, wd[...], preferred_element_type=jnp.float32).astype(jnp.bfloat16)
        for j in range(4):
            o = g * 4 + j

            @pl.when(o > 0)
            def _():
                ex_copy(o, 0, 1 - odd).start()
                ex_copy(o, 1, 1 - odd).start()

    def ret_copy(o, device):
        at = pl.ds(al(o * half_cap, half_cap), half_cap)
        return send(half_buf.at[at], ret.at[at], rt_s.at[o], rt_r.at[o], device)

    def give_back(g):
        for j in range(4):
            o = g * 4 + j

            @pl.when(o > 0)
            def _():
                ex_copy(o, 0, odd).wait_recv()
                ex_copy(o, 1, odd).wait_recv()
                own = part[pl.ds(al(o * cap + odd * half_cap, half_cap), half_cap), :]
                at = pl.ds(al(o * half_cap, half_cap), half_cap)
                half_buf[at, :] = (own.astype(jnp.float32) + yr[at, :].astype(jnp.float32)).astype(jnp.bfloat16)
                ret_copy(o, (source_at(g, j), y, c)).start()

    def split(value):
        high = value.astype(jnp.bfloat16)
        return high, (value - high.astype(jnp.float32)).astype(jnp.bfloat16)

    def spread(picker, values):
        high, low = split(picker)
        both = jnp.concatenate([high, low], axis=1)
        wide = lax.dot_general(both, values, TN, preferred_element_type=jnp.float32)
        return wide[:tokens] + wide[tokens:]

    half_id = (lax.broadcasted_iota(jnp.int32, (half_cap, tokens), 0) + odd * half_cap).astype(jnp.float32)

    def combine(g):
        @pl.when(g == 0)
        def _():
            ret[0:half_cap, :] = jnp.zeros((half_cap, width), jnp.bfloat16)
            picker = jnp.where(slots[pl.ds(me, 1), :] == slot_id, shares[pl.ds(me, 1), :], 0.0)
            acc[...] = spread(picker, part[0:cap, :])

        pickers = []
        for j in range(4):
            o = g * 4 + j

            @pl.when(o > 0)
            def _():
                ret_copy(o, (me, y, c)).wait_recv()

            e = expert_at(g, j)
            pickers.append(jnp.where(slots[pl.ds(e, 1), :] == half_id, shares[pl.ds(e, 1), :], 0.0))
        at = pl.ds(al(g * half_rows, half_rows), half_rows)
        acc[...] += spread(jnp.concatenate(pickers, axis=0), ret[at, :])

    load_wgu.wait()
    load_wd.wait()

    def step(i, _):
        @pl.when(i < GROUPS)
        def _():
            forward(i)

        @pl.when(jnp.logical_and(i >= 1, i < GROUPS + 1))
        def _():
            experts_of(i - 1)

        @pl.when(jnp.logical_and(i >= 2, i < GROUPS + 2))
        def _():
            give_back(i - 2)

        @pl.when(i >= 4)
        def _():
            combine(i - 4)

        return 0

    lax.fori_loop(0, GROUPS + 4, step, 0)

    if last:
        for q in range(SIDE):
            rs_send[q] = acc[:, q * share_width : (q + 1) * share_width].astype(jnp.bfloat16)
    else:
        rs_send[...] = acc[...].astype(jnp.bfloat16)
    portion = tokens // SIDE

    def rs_copy(k):
        to = (y + k) % SIDE
        src = rs_send.at[to] if last else rs_send.at[pl.ds(al(to * portion, portion), portion)]
        return send(src, rs_recv.at[k - 1], rs_s.at[k - 1], rs_r.at[k - 1], (me, to, c))

    for k in range(1, SIDE):
        rs_copy(k).start()
    if not last:
        total = cnt_r_buf[0]
        for o in range(1, 16):
            count_copy(o, (me, y, c)).wait_recv()
            total = total + cnt_r_buf[o]
        pair_s_buf[...] = total
        pair = send(pair_s_buf, pair_r_buf, cs.at[0], cr.at[0], (me, y, 1 - c))
        pair.start()
    for k in range(1, SIDE):
        rs_copy(k).wait_recv()
    if last:
        others = rs_recv[0].astype(jnp.float32) + rs_recv[1].astype(jnp.float32) + rs_recv[2].astype(jnp.float32)
        for q in range(SIDE):

            @pl.when(y == q)
            def _():
                cols = slice(q * share_width, (q + 1) * share_width)
                out_ref[...] = (x_ref[:, cols].astype(jnp.float32) + (acc[:, cols] + others)).astype(jnp.bfloat16)
    else:
        mine = pl.ds(al(y * portion, portion), portion)
        others = rs_recv[0].astype(jnp.float32) + rs_recv[1].astype(jnp.float32) + rs_recv[2].astype(jnp.float32)
        gathered[mine, :] = (x_ref[mine, :].astype(jnp.float32) + (acc[mine, :] + others)).astype(jnp.bfloat16)

        def ag_copy(k, owner):
            at = pl.ds(al(owner * portion, portion), portion)
            return send(gathered.at[at], gathered.at[at], ag_s.at[k - 1], ag_r.at[k - 1], (me, (y + k) % SIDE, c))

        for k in range(1, SIDE):
            ag_copy(k, y).start()
        pair.wait_recv()
        load_ref[...] = pair_s_buf[...] + pair_r_buf[...]
        for k in range(1, SIDE):
            ag_copy(k, (y - k + SIDE) % SIDE).wait_recv()
        out_ref[...] = gathered[...]

    def drain(o, _):
        @pl.when(o > 0)
        def _():
            in_copy(o // 4, o % 4, (me, y, c)).wait_send()
            fw_copy(o, 0, odd).wait_send()
            fw_copy(o, 1, odd).wait_send()
            ex_copy(o, 0, 1 - odd).wait_send()
            ex_copy(o, 1, 1 - odd).wait_send()
            ret_copy(o, (me, y, c)).wait_send()
            if not last:
                count_copy(o, (me, y, c)).wait_send()

        return 0

    lax.fori_loop(0, 16, drain, 0)
    for k in range(1, SIDE):
        rs_copy(k).wait_send()
        if not last:
            ag_copy(k, y).wait_send()
    if not last:
        pair.wait_send()


def layer(last, x, routes, shares, gains, gate_up, down, more_routes=None):
    tokens, width = x.shape
    ex = lax.axis_size("ex")
    top = routes.shape[1]
    share_width = down.shape[1]
    cap = 2 * tokens * top // ex
    slots = ex * cap
    bf, f32, i32 = jnp.bfloat16, jnp.float32, jnp.int32
    wgu = jnp.transpose(gate_up[0], (1, 2, 0)).reshape(2 * share_width, width)
    wd = down[0]
    vmem = pl.BlockSpec(memory_space=pltpu.VMEM)
    hbm = pl.BlockSpec(memory_space=pl.ANY)
    small = [x, routes.T] + ([] if last else [more_routes.T]) + [shares.T, gains.reshape(1, width)]
    rs_shape = (SIDE, tokens, share_width) if last else (tokens, width)
    rr_shape = (SIDE - 1, tokens, share_width) if last else (SIDE - 1, tokens // SIDE, width)
    dma = pltpu.SemaphoreType.DMA
    scratch = [
        pltpu.VMEM((2 * share_width, width), bf),
        pltpu.VMEM((share_width, width), bf),
        pltpu.VMEM((tokens, width), bf),
        pltpu.VMEM((ex, tokens), f32),
        pltpu.VMEM((ex, tokens), f32),
        pltpu.VMEM((slots, width), bf),
        pltpu.VMEM((slots, width), bf),
        pltpu.VMEM((slots, width), bf),
        pltpu.VMEM((slots // 2, width), bf),
        pltpu.VMEM((slots // 2, width), bf),
        pltpu.VMEM((slots // 2, width), bf),
        pltpu.VMEM((tokens, width), f32),
        pltpu.VMEM(rs_shape, bf),
        pltpu.VMEM(rr_shape, bf),
        dma((2,)),
        dma((16,)), dma((16,)),
        dma((16, 2)), dma((16, 2)),
        dma((16, 2)), dma((16, 2)),
        dma((16,)), dma((16,)),
        dma((3,)), dma((3,)),
    ]
    out_shape = [jax.ShapeDtypeStruct((tokens, share_width if last else width), bf)]
    if not last:
        out_shape.append(jax.ShapeDtypeStruct((8, 128), i32))
        scratch += [
            pltpu.VMEM((2, ex, tokens), f32),
            pltpu.VMEM((16, 8, 128), i32),
            pltpu.VMEM((16, 8, 128), i32),
            pltpu.VMEM((8, 128), i32),
            pltpu.VMEM((8, 128), i32),
            pltpu.VMEM((tokens, width), bf),
            dma((16,)), dma((16,)), dma((3,)), dma((3,)),
        ]
    return pl.pallas_call(
        functools.partial(layer_kernel, last, cap),
        name="layer_two" if last else "layer_one",
        out_shape=out_shape,
        in_specs=[vmem] * len(small) + [hbm, hbm],
        out_specs=[vmem] * len(out_shape),
        scratch_shapes=scratch,
        compiler_params=pltpu.CompilerParams(
            collective_id=1 if last else 0, has_side_effects=True, vmem_limit_bytes=64 * 1024 * 1024 - 65536
        ),
    )(*small, wgu, wd)


def body(
    tokens, route_one, route_two, share_one, share_two, gain_one, gain_two, gate_up_one, down_one, gate_up_two, down_two
):
    stream, load = layer(False, tokens, route_one, share_one, gain_one, gate_up_one, down_one, route_two)
    (mixed,) = layer(True, stream, route_two, share_two, gain_two, gate_up_two, down_two)
    return mixed, load[0:2, 0:1]


def solution(mesh):
    in_specs = (
        P(("ex", "dp"), None),
        P(("ex", "dp"), None),
        P(("ex", "dp"), None),
        P(("ex", "dp"), None),
        P(("ex", "dp"), None),
        P(),
        P(),
        P("ex", None, None, "tp"),
        P("ex", "tp", None),
        P("ex", None, None, "tp"),
        P("ex", "tp", None),
    )
    out_specs = (P(("ex", "dp"), "tp"), P(None, "ex"))
    return jax.shard_map(body, mesh=mesh, in_specs=in_specs, out_specs=out_specs, check_vma=False)
```

time: 519 us -> 234 us (0.45)
  Pallas kernels: 0 us -> 225 us
  blocking collectives: 169 us -> 0 us
  waiting for transfers between devices: 168 us -> 0 us
  local copies, waits for them, and re-layouts: 69.4 us -> 7.92 us
  matrix products: 51 us -> 0 us
  starting transfers between devices: 32.4 us -> 0 us
  other arithmetic: 25.7 us -> 0 us
    pallas_call x0 -> x2, Pallas kernels: none -> 225 us  [layer(): pl.pallas_call(functools.partial(layer_kernel, last, cap), name='layer_tw...]
    all_to_all x6 -> x0, waiting for transfers between devices: 168 us -> none  [the longest x1 71.2 us: expert_layer(): lax.all_to_all(packed, 'ex', split_axis=0, concat_axis=0, tiled=True)]
    all_to_all x2 -> x0, blocking collectives: 153 us -> none  [the longest x1 79.3 us: expert_layer(): lax.all_to_all(packed, 'ex', split_axis=0, concat_axis=0, tiled=True)]
    dot_general x6 -> x0, matrix products: 51 us -> none  [the longest x2 26.9 us: expert_layer(): jnp.einsum('secd,edf->secf', arrived, gate_up_flat, preferred_element_typ...]
    reshape x4 -> x2, local copies, waits for them, and re-layouts: 40.9 us -> 2.63 us  [layer(): gains.reshape(1, width)]
    all_to_all x6 -> x0, starting transfers between devices: 32.4 us -> none  [the longest x2 12.7 us: expert_layer(): lax.all_to_all(counts_out, 'ex', split_axis=0, concat_axis=0, tiled=True)]
    convert_element_type x5 -> x0, local copies, waits for them, and re-layouts: 18.1 us -> none  [the longest x2 17 us: pack_rows(): jnp.dot(chooser, normed, preferred_element_type=jnp.float32)]
    reduce_sum x10 -> x0, other arithmetic: 15.3 us -> none  [the longest x2 11.2 us: sent_and_summed(): return jnp.sum(pieces.astype(jnp.float32), axis=0)]
  transfers between devices with their start and end apart: 6 -> 0, of which waited for: 5 -> 0; matrix products, arithmetic and copies ran while one was open for 11% -> 0% of each run, Pallas kernels for 0% -> 0%
where the time goes in v1:
time: 234 us
  Pallas kernels  225 us (96%)
  local copies, waits for them, and re-layouts  7.92 us (3%)
    pallas_call x2, Pallas kernels, layer(): pl.pallas_call(functools.partial(layer_kernel, last, cap), name='layer_tw...  225 us

profile of v1, /device:TPU:0, one launch (start us, length us, event | category | flops | bytes accessed | tf_op | source)
XLA Modules:
  0.0 233.6 jit_solution(12270128065664049511)
XLA Ops:
  0.6 2.3 copy.13.refs_0_
  2.9 1.3 reshape.16.refs_4_
  4.2 118.5 %layer_one.1 = (bf16[128,2880]{1,0:T(8,128)(2,1)}, s32[8,128]{1,0:T(8,128)}) custom-call(bf16[128,2880]{1,0:T(8,128)(2,1)} %copy.13.refs_0_, s32[4,128]{1,0:T(4,128)} %bitcast.22, s32[4,128]{1,0:T(4,128)} %bitcast.20, f32[4,128]{1,0:T(4,128)} %bitcast.23, f32[1,2880]{1,0:T(1,128)} %reshape.16.refs_4_, bf16[1440,2880]{1,0:T(8,128)(2,1)} %bitcast.16, ...), custom_call_target="tpu_custom_call" | custom-call | tf_op jit(solution)/shard_map/layer_one/pallas_call | solution.py:388
  122.8 1.3 reshape.18.refs_3_
  124.1 106.5 %layer_two.1 = bf16[128,720]{1,0:T(8,128)(2,1)} custom-call(bf16[128,2880]{1,0:T(8,128)(2,1)} %get-tuple-element.4.refs_0_, s32[4,128]{1,0:T(4,128)} %bitcast.21, f32[4,128]{1,0:T(4,128)} %bitcast.24, f32[1,2880]{1,0:T(1,128)} %reshape.18.refs_3_, bf16[1440,2880]{1,0:T(8,128)(2,1)} %bitcast.17, bf16[720,2880]{1,0:T(8,128)(2,1)} %bitcast.19), custom_call_target="tpu_custom_call" | custom-call | tf_op jit(solution)/shard_map/layer_two/pallas_call | solution.py:388
  230.6 1.7 copy.14
  232.3 0.7 slice.3
  233.0 0.6 copy.15

commit v2 on v0

v2 whole, which is shorter than its diff:
```python
import functools

import jax
import jax.numpy as jnp
from jax import lax
from jax.experimental import pallas as pl
from jax.experimental.pallas import tpu as pltpu
from jax.sharding import PartitionSpec as P

MESH = pl.DeviceIdType.MESH
norm_eps = 1e-05
glu_alpha = 1.702
SIDE = 4
GROUPS = 4
OFFSETS = (
    (0, 0), (2, 2), (1, 1), (3, 3),
    (1, 3), (3, 1), (2, 1), (2, 3),
    (1, 2), (3, 2), (2, 0), (0, 2),
    (1, 0), (3, 0), (0, 1), (0, 3),
)
MODES_IN = "DQHHHHQQHHHHDDDD"
MODES_OUT = "DQHHHHQQHHHHDDDD"
COLUMNS = 1536
NT = (((1,), (1,)), ((), ()))
TN = (((0,), (0,)), ((), ()))
BF, F32, I32 = jnp.bfloat16, jnp.float32, jnp.int32


def al(v, m):
    return pl.multiple_of(v, m)


def moe_kernel(cap, *refs):
    (
        xt_ref, rt1_ref, rt2_ref, st1_ref, st2_ref, gain1_ref, gain2_ref, wgu1, wd1, wgu2, wd2, out_ref, load_ref,
        wgu, wd, x_buf, normed, hits, slots, shares, pk, arr, part, yr, half_buf, ret, acc, rs1_send, rs1_recv,
        rs2_send, rs2_recv, cnt_s_buf, cnt_r_buf, pair_s_buf, pair_r_buf,
        gains, w_sem, in_s, in_r, fw_s, fw_r, ex_s, ex_r, rt_s, rt_r, rs_s, rs_r, ag_s, ag_r, cs, cr,
    ) = refs
    width, tokens = xt_ref.shape
    share_width = wd.shape[0]
    half_cap = cap // 2
    quarter = cap // 4
    rows = 4 * cap
    portion = tokens // SIDE
    parts = ((0, COLUMNS), (COLUMNS, width - COLUMNS))
    cols = tuple(pl.ds(*p) for p in parts)

    me = lax.axis_index("ex")
    y = lax.axis_index("tp")
    c = lax.axis_index("dp")
    my_x, my_z = me // SIDE, me % SIDE
    odd = y % 2
    near = (y + 1 - 2 * odd + SIDE) % SIDE
    far = (y - 1 + 2 * odd + SIDE) % SIDE
    partners = (near, far, (y + 2) % SIDE)

    def expert_at(o):
        dx, dz = OFFSETS[o]
        return ((my_x + dx) % SIDE) * SIDE + (my_z + dz) % SIDE

    def source_at(o):
        dx, dz = OFFSETS[o]
        return ((my_x - dx + SIDE) % SIDE) * SIDE + (my_z - dz + SIDE) % SIDE

    def send(src, dst, s_sem, r_sem, device):
        return pltpu.make_async_remote_copy(
            src_ref=src, dst_ref=dst, send_sem=s_sem, recv_sem=r_sem, device_id=device, device_id_type=MESH
        )

    barrier = pltpu.get_barrier_semaphore()
    for o in range(1, 16):
        pl.semaphore_signal(barrier, inc=1, device_id=(expert_at(o), y, c), device_id_type=MESH)
    for k in range(1, SIDE):
        pl.semaphore_signal(barrier, inc=1, device_id=(me, (y + k) % SIDE, c), device_id_type=MESH)
    pl.semaphore_signal(barrier, inc=1, device_id=(me, y, 1 - c), device_id_type=MESH)

    def weights(gu, down):
        return pltpu.make_async_copy(gu, wgu, w_sem.at[0]), pltpu.make_async_copy(down, wd, w_sem.at[1])

    for load in weights(wgu1, wd1):
        load.start()

    experts = slots.shape[1]
    expert_id = lax.broadcasted_iota(I32, (experts, tokens), 0)
    before = lax.broadcasted_iota(I32, (tokens, tokens), 0) < lax.broadcasted_iota(I32, (tokens, tokens), 1)
    before = jnp.where(before, 1.0, 0.0).astype(BF)
    for level, (rt_ref, st_ref) in enumerate(((rt1_ref, st1_ref), (rt2_ref, st2_ref))):
        table = rt_ref[...]
        hit = jnp.zeros((experts, tokens), F32)
        weight = jnp.zeros((experts, tokens), F32)
        for k in range(table.shape[0]):
            same = table[k : k + 1, :] == expert_id
            hit = hit + jnp.where(same, 1.0, 0.0)
            weight = weight + jnp.where(same, st_ref[k : k + 1, :], 0.0)
        rank = jnp.dot(hit.astype(BF), before, preferred_element_type=F32)
        hits[level] = hit
        slots[level] = jnp.where(hit > 0.5, rank, -1.0)
        shares[level] = weight

    lane_id = lax.broadcasted_iota(I32, (8, 128), 1)

    def count_tile(e):
        one = jnp.sum(hits[0, pl.ds(e, 1), :], axis=1, keepdims=True)
        two = jnp.sum(hits[1, pl.ds(e, 1), :], axis=1, keepdims=True)
        return jnp.where(lane_id == 0, one, jnp.where(lane_id == 1, two, 0.0)).astype(I32)

    def count_copy(o, device):
        return send(cnt_s_buf.at[o], cnt_r_buf.at[o], cs.at[o], cr.at[o], device)

    pair = send(pair_s_buf, pair_r_buf, cs.at[0], cr.at[0], (me, y, 1 - c))

    for k in range(0, width, 128):
        wide = min(128, width - k)
        x_buf[:, k : k + wide] = xt_ref[k : k + wide, :].astype(F32).T.astype(BF)

    gains[0] = gain1_ref[...].reshape(1, width)
    gains[1] = gain2_ref[...].reshape(1, width)
    slot_id = lax.broadcasted_iota(I32, (cap, tokens), 0).astype(F32)
    half_id = (lax.broadcasted_iota(I32, (half_cap, tokens), 0) + odd * half_cap).astype(F32)
    quarter_id = (lax.broadcasted_iota(I32, (quarter, tokens), 0) + y * quarter).astype(F32)
    kept = {"D": cap, "H": half_cap, "Q": quarter}
    ids = {"D": slot_id, "H": half_id, "Q": quarter_id}
    swaps = {"D": 0, "H": 2, "Q": 3}

    def split(value):
        high = value.astype(BF)
        return high, (value - high.astype(F32)).astype(BF)

    def spread(picker, values):
        high, low = split(picker)
        both = jnp.concatenate([high, low], axis=1)
        wide = lax.dot_general(both, values, TN, preferred_element_type=F32)
        return wide[:tokens] + wide[tokens:]

    def own_rows(mode, o):
        start = {"D": 0, "H": odd * half_cap, "Q": y * quarter}[mode]
        return pl.ds(al(o * cap + start, kept[mode]), kept[mode])

    def swap_rows(mode, o, j, mine):
        if mode == "H":
            return pl.ds(al(o * cap + (odd if mine else 1 - odd) * half_cap + j * quarter, quarter), quarter)
        return pl.ds(al(o * cap + (y if mine else partners[j]) * quarter, quarter), quarter)

    def in_copy(o, device):
        at = own_rows(MODES_IN[o], o)
        return send(pk.at[at], arr.at[at], in_s.at[o], in_r.at[o], device)

    def fw_copy(o, j, mine):
        at = swap_rows(MODES_IN[o], o, j, mine)
        return send(arr.at[at], arr.at[at], fw_s.at[o, j], fw_r.at[o, j], (me, partners[j], c))

    def ex_rows(o, j):
        return pl.ds((o * 3 + j) * quarter, quarter)

    def ex_copy(o, j, h):
        src = swap_rows(MODES_OUT[o], o, j, False)
        return send(
            part.at[src, cols[h]], yr.at[ex_rows(o, j), cols[h]], ex_s.at[o, j, h], ex_r.at[o, j, h], (me, partners[j], c)
        )

    def ret_rows(o):
        return pl.ds(o * cap, kept[MODES_OUT[o]])

    def ret_copy(o, h, device):
        if MODES_OUT[o] == "D":
            src = part.at[pl.ds(o * cap, cap), cols[h]]
        else:
            src = half_buf.at[pl.ds(o * half_cap, kept[MODES_OUT[o]]), cols[h]]
        return send(src, ret.at[ret_rows(o), cols[h]], rt_s.at[o, h], rt_r.at[o, h], device)

    def group(g):
        return range(4 * g, 4 * g + 4)

    def forward(g):
        for o in group(g):
            if o > 0:
                in_copy(o, (me, y, c)).wait_recv()
                for j in range(swaps[MODES_IN[o]]):
                    fw_copy(o, j, True).start()

    def experts_of(g):
        for o in group(g):
            for j in range(swaps[MODES_IN[o]]):
                fw_copy(o, j, False).wait_recv()
        at = slice(g * rows, (g + 1) * rows)
        inputs = arr[at, :]
        gate = lax.dot_general(inputs, wgu[0:share_width, :], NT, preferred_element_type=F32)
        up = lax.dot_general(inputs, wgu[share_width:, :], NT, preferred_element_type=F32)
        act = (gate * jax.nn.sigmoid(glu_alpha * gate) * (up + 1.0)).astype(BF)
        part[at, :] = jnp.dot(act, wd[...], preferred_element_type=F32).astype(BF)
        for o in group(g):
            for j in range(swaps[MODES_IN[o]]):
                fw_copy(o, j, True).wait_send()
        for h in range(2):
            for o in group(g):
                if o > 0 and MODES_OUT[o] == "D":
                    ret_copy(o, h, (source_at(o), y, c)).start()
                for j in range(swaps[MODES_OUT[o]]):
                    ex_copy(o, j, h).start()

    def give_back(g, h):
        for o in group(g):
            mode = MODES_OUT[o]
            if mode == "D":
                continue
            total = part[own_rows(mode, o), cols[h]].astype(F32)
            got = []
            for j in range(swaps[mode]):
                ex_copy(o, j, h).wait_recv()
                got.append(yr[ex_rows(o, j), cols[h]].astype(F32))
            if mode == "H":
                total = total + jnp.concatenate(got, axis=0)
            else:
                total = total + got[0] + got[1] + got[2]
            half_buf[pl.ds(o * half_cap, kept[mode]), cols[h]] = total.astype(BF)
            ret_copy(o, h, (source_at(o), y, c)).start()

    def combine(slot, share, g, h):
        pickers, values = [], []
        for o in group(g):
            e = expert_at(o)
            if o == 0:
                values.append(part[0:cap, cols[h]])
            else:
                ret_copy(o, h, (me, y, c)).wait_recv()
                values.append(ret[ret_rows(o), cols[h]])
            pickers.append(jnp.where(slot[pl.ds(e, 1), :] == ids[MODES_OUT[o]], share[pl.ds(e, 1), :], 0.0))
        total = spread(jnp.concatenate(pickers, axis=0), jnp.concatenate(values, axis=0))
        if g == 0:
            acc[:, cols[h]] = total
        else:
            acc[:, cols[h]] += total

    def rs1_copy(k, h):
        to = (y + k) % SIDE
        src = rs1_send.at[pl.ds(al(to * portion, portion), portion), cols[h]]
        return send(src, rs1_recv.at[k - 1, :, cols[h]], rs_s.at[h, k - 1], rs_r.at[h, k - 1], (me, to, c))

    def rs2_copy(k, to):
        return send(rs2_send.at[to], rs2_recv.at[k - 1], rs_s.at[2, k - 1], rs_r.at[2, k - 1], (me, to, c))

    def ag_copy(k, owner, h):
        at = pl.ds(al(owner * portion, portion), portion)
        there = x_buf.at[at, cols[h]]
        return send(there, there, ag_s.at[h, k - 1], ag_r.at[h, k - 1], (me, (y + k) % SIDE, c))

    def sent_all():
        for o in range(1, 16):
            in_copy(o, (me, y, c)).wait_send()
            for h in range(2):
                for j in range(swaps[MODES_OUT[o]]):
                    ex_copy(o, j, h).wait_send()
                ret_copy(o, h, (me, y, c)).wait_send()

    def rs_start(first, h):
        @pl.when(first)
        def _():
            rs1_send[:, cols[h]] = acc[:, cols[h]].astype(BF)
            for k in range(1, SIDE):
                rs1_copy(k, h).start()

        @pl.when(jnp.logical_not(first))
        def _():
            for q in (2 * h, 2 * h + 1):
                rs2_send[q] = acc[:, q * share_width : (q + 1) * share_width].astype(BF)

                @pl.when(y != q)
                def _():
                    rs2_copy((q - y + SIDE) % SIDE, q).start()

    def layer(level, _):
        first = level == 0
        slot = slots.at[level]
        share = shares.at[level]

        gain = gains[level]
        for r in range(0, tokens, 16):
            v = x_buf[r : r + 16, :].astype(F32)
            inverse = lax.rsqrt(jnp.mean(v * v, axis=1, keepdims=True) + norm_eps)
            normed[r : r + 16, :] = (v * inverse * gain).astype(BF)

        @pl.when(first)
        def _():
            pl.semaphore_wait(barrier, 19)

        for g in range(GROUPS):
            chooser = jnp.concatenate(
                [jnp.where(slot[pl.ds(expert_at(o), 1), :] == slot_id, 1.0, 0.0) for o in group(g)], axis=0
            ).astype(BF)
            packed = jnp.dot(chooser, normed[...], preferred_element_type=F32).astype(BF)
            pk[g * rows : (g + 1) * rows, :] = packed
            if g == 0:
                arr[0:cap, :] = packed[0:cap]
            for o in group(g):
                if o > 0:
                    in_copy(o, (expert_at(o), y, c)).start()

        @pl.when(first)
        def _():
            cnt_r_buf[0] = count_tile(me)
            for o in range(1, 16):
                cnt_s_buf[o] = count_tile(expert_at(o))
                count_copy(o, (expert_at(o), y, c)).start()

        for load in weights(wgu1, wd1):
            load.wait()
        forward(0)
        forward(1)
        experts_of(0)
        forward(2)
        experts_of(1)
        forward(3)
        give_back(0, 0)
        give_back(0, 1)
        experts_of(3)
        experts_of(2)

        @pl.when(first)
        def _():
            for load in weights(wgu2, wd2):
                load.start()

        give_back(1, 0)
        give_back(1, 1)
        combine(slot, share, 0, 0)
        give_back(2, 0)
        combine(slot, share, 3, 0)
        combine(slot, share, 1, 0)
        give_back(2, 1)
        combine(slot, share, 2, 0)
        rs_start(first, 0)
        combine(slot, share, 0, 1)
        combine(slot, share, 3, 1)
        combine(slot, share, 1, 1)
        combine(slot, share, 2, 1)
        rs_start(first, 1)

        @pl.when(first)
        def _():
            mine = pl.ds(al(y * portion, portion), portion)
            for h in range(2):
                for k in range(1, SIDE):
                    rs1_copy(k, h).wait_recv()
                others = rs1_recv[0, :, cols[h]].astype(F32)
                for k in range(1, SIDE - 1):
                    others = others + rs1_recv[k, :, cols[h]].astype(F32)
                x_buf[mine, cols[h]] = (x_buf[mine, cols[h]].astype(F32) + (acc[mine, cols[h]] + others)).astype(BF)
                for k in range(1, SIDE):
                    ag_copy(k, y, h).start()
                if h == 0:
                    total = cnt_r_buf[0]
                    for o in range(1, 16):
                        count_copy(o, (me, y, c)).wait_recv()
                        total = total + cnt_r_buf[o]
                    pair_s_buf[...] = total
                    pair.start()
                    sent_all()
                    for o in range(1, 16):
                        count_copy(o, (me, y, c)).wait_send()
            pair.wait_recv()
            load_ref[...] = (pair_s_buf[...] + pair_r_buf[...])[0:1, 0:2]
            pair.wait_send()
            for h in range(2):
                for k in range(1, SIDE):
                    rs1_copy(k, h).wait_send()
                    ag_copy(k, (y - k + SIDE) % SIDE, h).wait_recv()
            for h in range(2):
                for k in range(1, SIDE):
                    ag_copy(k, y, h).wait_send()

        @pl.when(level == 1)
        def _():
            sent_all()
            for k in range(1, SIDE):
                rs2_copy(k, y).wait_recv()
            others = rs2_recv[0].astype(F32) + rs2_recv[1].astype(F32) + rs2_recv[2].astype(F32)
            for q in range(SIDE):

                @pl.when(y == q)
                def _():
                    own = slice(q * share_width, (q + 1) * share_width)
                    out_ref[...] = (x_buf[:, own].astype(F32) + (acc[:, own] + others)).T.astype(BF)

            for k in range(1, SIDE):
                rs2_copy(k, (y + k) % SIDE).wait_send()

        return 0

    lax.fori_loop(0, 2, layer, 0)


def body(
    tokens, route_one, route_two, share_one, share_two, gain_one, gain_two, gate_up_one, down_one, gate_up_two, down_two
):
    count, width = tokens.shape
    ex = lax.axis_size("ex")
    top = route_one.shape[1]
    share_width = down_one.shape[1]
    cap = 2 * count * top // ex
    total = ex * cap
    vmem = pl.BlockSpec(memory_space=pltpu.VMEM)
    hbm = pl.BlockSpec(memory_space=pl.ANY)
    dma = pltpu.SemaphoreType.DMA

    def flat(gate_up):
        return jnp.transpose(gate_up[0], (1, 2, 0)).reshape(2 * share_width, width)

    mixed, load = pl.pallas_call(
        functools.partial(moe_kernel, cap),
        name="two_layers",
        out_shape=[jax.ShapeDtypeStruct((share_width, count), BF), jax.ShapeDtypeStruct((1, 2), I32)],
        in_specs=[vmem] * 7 + [hbm] * 4,
        out_specs=[vmem] * 2,
        scratch_shapes=[
            pltpu.VMEM((2 * share_width, width), BF),
            pltpu.VMEM((share_width, width), BF),
            pltpu.VMEM((count, width), BF),
            pltpu.VMEM((count, width), BF),
            pltpu.VMEM((2, ex, count), F32),
            pltpu.VMEM((2, ex, count), F32),
            pltpu.VMEM((2, ex, count), F32),
            pltpu.VMEM((total, width), BF),
            pltpu.VMEM((total, width), BF),
            pltpu.VMEM((total, width), BF),
            pltpu.VMEM((total * 3 // 4, width), BF),
            pltpu.VMEM((total // 2, width), BF),
            pltpu.VMEM((total, width), BF),
            pltpu.VMEM((count, width), F32),
            pltpu.VMEM((count, width), BF),
            pltpu.VMEM((SIDE - 1, count // SIDE, width), BF),
            pltpu.VMEM((SIDE, count, share_width), BF),
            pltpu.VMEM((SIDE - 1, count, share_width), BF),
            pltpu.VMEM((16, 8, 128), I32),
            pltpu.VMEM((16, 8, 128), I32),
            pltpu.VMEM((8, 128), I32),
            pltpu.VMEM((8, 128), I32),
            pltpu.VMEM((2, 1, width), F32),
            dma((2,)),
            dma((16,)), dma((16,)),
            dma((16, 3)), dma((16, 3)),
            dma((16, 3, 2)), dma((16, 3, 2)),
            dma((16, 2)), dma((16, 2)),
            dma((3, 3)), dma((3, 3)),
            dma((2, 3)), dma((2, 3)),
            dma((16,)), dma((16,)),
        ],
        compiler_params=pltpu.CompilerParams(
            collective_id=0, has_side_effects=True, vmem_limit_bytes=64 * 1024 * 1024 - 65536
        ),
    )(
        tokens.T, route_one.T, route_two.T, share_one.T, share_two.T, gain_one, gain_two,
        flat(gate_up_one), down_one[0], flat(gate_up_two), down_two[0],
    )
    return mixed.T, load.T


def solution(mesh):
    in_specs = (
        P(("ex", "dp"), None),
        P(("ex", "dp"), None),
        P(("ex", "dp"), None),
        P(("ex", "dp"), None),
        P(("ex", "dp"), None),
        P(),
        P(),
        P("ex", None, None, "tp"),
        P("ex", "tp", None),
        P("ex", None, None, "tp"),
        P("ex", "tp", None),
    )
    out_specs = (P(("ex", "dp"), "tp"), P(None, "ex"))
    return jax.shard_map(body, mesh=mesh, in_specs=in_specs, out_specs=out_specs, check_vma=False)
```

time: 519 us -> 193 us (0.37)
  Pallas kernels: 0 us -> 190 us
  blocking collectives: 169 us -> 0 us
  waiting for transfers between devices: 168 us -> 0 us
  local copies, waits for them, and re-layouts: 69.4 us -> 2.74 us
  matrix products: 51 us -> 0 us
  starting transfers between devices: 32.4 us -> 0 us
  other arithmetic: 25.7 us -> 0 us
    pallas_call x0 -> x1, Pallas kernels: none -> 190 us  [body(): pl.pallas_call(functools.partial(moe_kernel, cap), name='two_layers', out...]
    all_to_all x6 -> x0, waiting for transfers between devices: 168 us -> none  [the longest x1 71.2 us: expert_layer(): lax.all_to_all(packed, 'ex', split_axis=0, concat_axis=0, tiled=True)]
    all_to_all x2 -> x0, blocking collectives: 153 us -> none  [the longest x1 79.3 us: expert_layer(): lax.all_to_all(packed, 'ex', split_axis=0, concat_axis=0, tiled=True)]
    dot_general x6 -> x0, matrix products: 51 us -> none  [the longest x2 26.9 us: expert_layer(): jnp.einsum('secd,edf->secf', arrived, gate_up_flat, preferred_element_typ...]
    reshape x4 -> x0, local copies, waits for them, and re-layouts: 40.9 us -> none  [cut_along(): return jnp.moveaxis(value.reshape(*before, length, -1, *after), dim, 0)]
    all_to_all x6 -> x0, starting transfers between devices: 32.4 us -> none  [the longest x2 12.7 us: expert_layer(): lax.all_to_all(counts_out, 'ex', split_axis=0, concat_axis=0, tiled=True)]
    convert_element_type x5 -> x0, local copies, waits for them, and re-layouts: 18.1 us -> none  [the longest x2 17 us: pack_rows(): jnp.dot(chooser, normed, preferred_element_type=jnp.float32)]
    reduce_sum x10 -> x0, other arithmetic: 15.3 us -> none  [the longest x2 11.2 us: sent_and_summed(): return jnp.sum(pieces.astype(jnp.float32), axis=0)]
  transfers between devices with their start and end apart: 6 -> 0, of which waited for: 5 -> 0; matrix products, arithmetic and copies ran while one was open for 11% -> 0% of each run, Pallas kernels for 0% -> 0%
where the time goes in v2:
time: 193 us
  Pallas kernels  190 us (98%)
  local copies, waits for them, and re-layouts  2.74 us (1%)
    pallas_call x1, Pallas kernels, body(): pl.pallas_call(functools.partial(moe_kernel, cap), name='two_layers', out...  190 us

profile of v2, /device:TPU:0, one launch (start us, length us, event | category | flops | bytes accessed | tf_op | source)
XLA Modules:
  0.0 192.9 jit_solution(798666138168719494)
XLA Ops:
  0.6 189.5 %two_layers.1 = (bf16[720,128]{1,0:T(8,128)(2,1)}, s32[1,2]{1,0:T(1,128)}) custom-call(bf16[2880,128]{1,0:T(8,128)(2,1)} %bitcast.23, s32[4,128]{1,0:T(4,128)} %bitcast.25, s32[4,128]{1,0:T(4,128)} %bitcast.26, f32[4,128]{1,0:T(4,128)} %bitcast.27, f32[4,128]{1,0:T(4,128)} %bitcast.28, f32[2880]{0:T(1024)} %refs_5_.1, f32[2880]{0:T(1024)} %refs_6_.1, ...), custom_call_target="tpu_custom_call" | custom-call | tf_op jit(solution)/shard_map/two_layers/pallas_call | solution.py:409
  190.2 1.6 copy.15
  191.8 1.1 copy.16

commit v3 on v2

--- a/solution.py
+++ b/solution.py
@@ -19,8 +19,8 @@
     (1, 0), (3, 0), (0, 1), (0, 3),
 )
 MODES_IN = "DQHHHHQQHHHHDDDD"
-MODES_OUT = "DQHHHHQQHHHHDDDD"
-COLUMNS = 1536
+MODES_OUT = "DQHHHHQQQQDDDDDD"
+COLUMNS = 2048
 NT = (((1,), (1,)), ((), ()))
 TN = (((0,), (0,)), ((), ()))
 BF, F32, I32 = jnp.bfloat16, jnp.float32, jnp.int32
@@ -179,7 +179,7 @@
                 for j in range(swaps[MODES_IN[o]]):
                     fw_copy(o, j, True).start()
 
-    def experts_of(g):
+    def experts_of(g, then):
         for o in group(g):
             for j in range(swaps[MODES_IN[o]]):
                 fw_copy(o, j, False).wait_recv()
@@ -192,8 +192,8 @@
         for o in group(g):
             for j in range(swaps[MODES_IN[o]]):
                 fw_copy(o, j, True).wait_send()
-        for h in range(2):
-            for o in group(g):
+        for p, h in then:
+            for o in group(p):
                 if o > 0 and MODES_OUT[o] == "D":
                     ret_copy(o, h, (source_at(o), y, c)).start()
                 for j in range(swaps[MODES_OUT[o]]):
@@ -269,6 +269,17 @@
                 def _():
                     rs2_copy((q - y + SIDE) % SIDE, q).start()
 
+    def summed(h):
+        mine = pl.ds(al(y * portion, portion), portion)
+        for k in range(1, SIDE):
+            rs1_copy(k, h).wait_recv()
+        others = rs1_recv[0, :, cols[h]].astype(F32)
+        for k in range(1, SIDE - 1):
+            others = others + rs1_recv[k, :, cols[h]].astype(F32)
+        x_buf[mine, cols[h]] = (x_buf[mine, cols[h]].astype(F32) + (acc[mine, cols[h]] + others)).astype(BF)
+        for k in range(1, SIDE):
+            ag_copy(k, y, h).start()
+
     def layer(level, _):
         first = level == 0
         slot = slots.at[level]
@@ -307,14 +318,14 @@
             load.wait()
         forward(0)
         forward(1)
-        experts_of(0)
+        experts_of(0, ((0, 0), (0, 1)))
         forward(2)
-        experts_of(1)
+        experts_of(1, ((1, 0),))
         forward(3)
         give_back(0, 0)
         give_back(0, 1)
-        experts_of(3)
-        experts_of(2)
+        experts_of(3, ((3, 0), (3, 1)))
+        experts_of(2, ((2, 0), (1, 1), (2, 1)))
 
         @pl.when(first)
         def _():
@@ -322,12 +333,12 @@
                 load.start()
 
         give_back(1, 0)
-        give_back(1, 1)
         combine(slot, share, 0, 0)
         give_back(2, 0)
+        give_back(1, 1)
+        give_back(2, 1)
         combine(slot, share, 3, 0)
         combine(slot, share, 1, 0)
-        give_back(2, 1)
         combine(slot, share, 2, 0)
         rs_start(first, 0)
         combine(slot, share, 0, 1)
@@ -338,26 +349,17 @@
 
         @pl.when(first)
         def _():
-            mine = pl.ds(al(y * portion, portion), portion)
-            for h in range(2):
-                for k in range(1, SIDE):
-                    rs1_copy(k, h).wait_recv()
-                others = rs1_recv[0, :, cols[h]].astype(F32)
-                for k in range(1, SIDE - 1):
-                    others = others + rs1_recv[k, :, cols[h]].astype(F32)
-                x_buf[mine, cols[h]] = (x_buf[mine, cols[h]].astype(F32) + (acc[mine, cols[h]] + others)).astype(BF)
-                for k in range(1, SIDE):
-                    ag_copy(k, y, h).start()
-                if h == 0:
-                    total = cnt_r_buf[0]
-                    for o in range(1, 16):
-                        count_copy(o, (me, y, c)).wait_recv()
-                        total = total + cnt_r_buf[o]
-                    pair_s_buf[...] = total
-                    pair.start()
-                    sent_all()
-                    for o in range(1, 16):
-                        count_copy(o, (me, y, c)).wait_send()
+            summed(0)
+            total = cnt_r_buf[0]
+            for o in range(1, 16):
+                count_copy(o, (me, y, c)).wait_recv()
+                total = total + cnt_r_buf[o]
+            pair_s_buf[...] = total
+            pair.start()
+            sent_all()
+            for o in range(1, 16):
+                count_copy(o, (me, y, c)).wait_send()
+            summed(1)
             pair.wait_recv()
             load_ref[...] = (pair_s_buf[...] + pair_r_buf[...])[0:1, 0:2]
             pair.wait_send()

time: 193 us -> 185 us (0.959)
  Pallas kernels: 190 us -> 180 us
    pallas_call x1, Pallas kernels: 190 us -> 180 us  [body(): pl.pallas_call(functools.partial(moe_kernel, cap), name='two_layers', out...]
where the time goes in v3:
time: 185 us; the launch traced here: 183 us
  Pallas kernels  180 us (97%)
  local copies, waits for them, and re-layouts  2.74 us (1%)
    pallas_call x1, Pallas kernels, body(): pl.pallas_call(functools.partial(moe_kernel, cap), name='two_layers', out...  180 us

profile of v3, /device:TPU:0, one launch (start us, length us, event | category | flops | bytes accessed | tf_op | source)
XLA Modules:
  0.0 183.1 jit_solution(18381574105688448795)
XLA Ops:
  0.6 179.7 %two_layers.1 = (bf16[720,128]{1,0:T(8,128)(2,1)}, s32[1,2]{1,0:T(1,128)}) custom-call(bf16[2880,128]{1,0:T(8,128)(2,1)} %bitcast.23, s32[4,128]{1,0:T(4,128)} %bitcast.25, s32[4,128]{1,0:T(4,128)} %bitcast.26, f32[4,128]{1,0:T(4,128)} %bitcast.27, f32[4,128]{1,0:T(4,128)} %bitcast.28, f32[2880]{0:T(1024)} %refs_5_.1, f32[2880]{0:T(1024)} %refs_6_.1, ...), custom_call_target="tpu_custom_call" | custom-call | tf_op jit(solution)/shard_map/two_layers/pallas_call | solution.py:411
  180.3 1.6 copy.15
  181.9 1.1 copy.16

commit v4 on v3

--- a/solution.py
+++ b/solution.py
@@ -20,7 +20,7 @@
 )
 MODES_IN = "DQHHHHQQHHHHDDDD"
 MODES_OUT = "DQHHHHQQQQDDDDDD"
-COLUMNS = 2048
+COLUMNS = 2304
 NT = (((1,), (1,)), ((), ()))
 TN = (((0,), (0,)), ((), ()))
 BF, F32, I32 = jnp.bfloat16, jnp.float32, jnp.int32
@@ -262,7 +262,7 @@
 
         @pl.when(jnp.logical_not(first))
         def _():
-            for q in (2 * h, 2 * h + 1):
+            for q in ((0, 1, 2), (3,))[h]:
                 rs2_send[q] = acc[:, q * share_width : (q + 1) * share_width].astype(BF)
 
                 @pl.when(y != q)
@@ -291,10 +291,6 @@
             inverse = lax.rsqrt(jnp.mean(v * v, axis=1, keepdims=True) + norm_eps)
             normed[r : r + 16, :] = (v * inverse * gain).astype(BF)
 
-        @pl.when(first)
-        def _():
-            pl.semaphore_wait(barrier, 19)
-
         for g in range(GROUPS):
             chooser = jnp.concatenate(
                 [jnp.where(slot[pl.ds(expert_at(o), 1), :] == slot_id, 1.0, 0.0) for o in group(g)], axis=0
@@ -303,6 +299,11 @@
             pk[g * rows : (g + 1) * rows, :] = packed
             if g == 0:
                 arr[0:cap, :] = packed[0:cap]
+
+                @pl.when(first)
+                def _():
+                    pl.semaphore_wait(barrier, 19)
+
             for o in group(g):
                 if o > 0:
                     in_copy(o, (expert_at(o), y, c)).start()
@@ -360,9 +361,6 @@
             for o in range(1, 16):
                 count_copy(o, (me, y, c)).wait_send()
             summed(1)
-            pair.wait_recv()
-            load_ref[...] = (pair_s_buf[...] + pair_r_buf[...])[0:1, 0:2]
-            pair.wait_send()
             for h in range(2):
                 for k in range(1, SIDE):
                     rs1_copy(k, h).wait_send()
@@ -390,6 +388,9 @@
         return 0
 
     lax.fori_loop(0, 2, layer, 0)
+    pair.wait_recv()
+    load_ref[...] = (pair_s_buf[...] + pair_r_buf[...])[0:1, 0:2]
+    pair.wait_send()
 
 
 def body(

time: 185 us -> 184 us (level)
  no operation moved by 1% of the time
where the time goes in v4:
time: 184 us; the launch traced here: 183 us
  Pallas kernels  180 us (98%)
  local copies, waits for them, and re-layouts  2.74 us (1%)
    pallas_call x1, Pallas kernels, body(): pl.pallas_call(functools.partial(moe_kernel, cap), name='two_layers', out...  180 us

profile of v4, /device:TPU:0, one launch (start us, length us, event | category | flops | bytes accessed | tf_op | source)
XLA Modules:
  0.0 183.0 jit_solution(18381569254339500513)
XLA Ops:
  0.6 179.7 %two_layers.1 = (bf16[720,128]{1,0:T(8,128)(2,1)}, s32[1,2]{1,0:T(1,128)}) custom-call(bf16[2880,128]{1,0:T(8,128)(2,1)} %bitcast.23, s32[4,128]{1,0:T(4,128)} %bitcast.25, s32[4,128]{1,0:T(4,128)} %bitcast.26, f32[4,128]{1,0:T(4,128)} %bitcast.27, f32[4,128]{1,0:T(4,128)} %bitcast.28, f32[2880]{0:T(1024)} %refs_5_.1, f32[2880]{0:T(1024)} %refs_6_.1, ...), custom_call_target="tpu_custom_call" | custom-call | tf_op jit(solution)/shard_map/two_layers/pallas_call | solution.py:412
  180.3 1.6 copy.15
  181.9 1.1 copy.16
